TPU v7x, 32 devices: a whole 2x2x4 slice. The times are simulated.
32 devices in a mesh: expert: 16 (over z, y, x), tensor: 2 (over core).
Axes of the slice: x: 2, y: 2, z: 4, core: 2. Of those that a mesh axis runs over, the one named last changes fastest.
Arguments:
- grad_out: bfloat16 [256, 3584], P('expert'), may hold values from -1.5 to 1.5
- expert_ids: int32 [256, 8], P('expert'), may hold values from 0 to 15, all different within a row; in each aligned block of 16 rows (0 to 15, 16 to 31, ...) at most 16 rows name the same one
- gate_values: float32 [256, 8], P('expert'), may hold values from 0.05 to 0.6
- w_gate_up: bfloat16 [16, 2, 3584, 1024], P('expert', None, None, 'tensor'), may hold values from -0.09375 to 0.09375
- w_down: bfloat16 [16, 1024, 3584], P('expert', 'tensor'), may hold values from -0.1875 to 0.1875
- saved_routed: bfloat16 [16, 2, 256, 1024], P('expert', None, None, 'tensor'), may hold values from -6 to 6
- shared_gate_up: bfloat16 [2, 3584, 1024], P(None, 'expert', 'tensor'), may hold values from -0.09375 to 0.09375
- shared_down: bfloat16 [1024, 3584], P('tensor', 'expert'), may hold values from -0.1875 to 0.1875
- saved_shared: bfloat16 [2, 256, 1024], P(None, 'expert', 'tensor'), may hold values from -6 to 6
Outputs:
- grad_in: bfloat16 [256, 3584], P('expert', 'tensor')
- grad_gates: float32 [256, 8], P('expert')
Inputs may be any that keep to these rules, and one draw needn't show every extreme that they name: `expert_ids`: each row names 8 different experts. Among the 16 rows of one index of expert (aligned blocks of rows), no expert is named by more than 16 rows, and in some block one expert is named by exactly 16 rows.
All inputs are finite; a program needn't handle non-finite values.
Results may differ from a plain program's by a relative error of at most 0.015.
Values may be sent and summed in bfloat16 or wider, within the bound.
A program may use at most 64 MiB of HBM per device.

v0:
```python
import jax
import jax.numpy as jnp
from jax import lax
from jax.sharding import PartitionSpec as P


def contract_last(left_side, right_side):
    return lax.dot_general(
        left_side, right_side, (((1,), (1,)), ((), ())), preferred_element_type=jnp.float32
    )


def swiglu_grads(back_grad, saved_gate, saved_up):
    pre_gate = saved_gate.astype(jnp.float32)
    pre_up = saved_up.astype(jnp.float32)
    sigmoid = jax.nn.sigmoid(pre_gate)
    grad_gate = (back_grad * pre_up * sigmoid * (1.0 + pre_gate * (1.0 - sigmoid))).astype(
        jnp.bfloat16
    )
    grad_up = (back_grad * pre_gate * sigmoid).astype(jnp.bfloat16)
    return (grad_gate, grad_up)


def gate_mixture(back_grad, saved_gate, saved_up):
    pre_gate = saved_gate.astype(jnp.float32)
    pre_up = saved_up.astype(jnp.float32)
    sigmoid = jax.nn.sigmoid(pre_gate)
    return back_grad * pre_gate * sigmoid * pre_up


def per_device(
    grad_out,
    expert_ids,
    gate_values,
    w_gate_up,
    w_down,
    saved_routed,
    shared_gate_up,
    shared_down,
    saved_shared,
):
    experts = lax.axis_size("expert")
    tokens, features = grad_out.shape
    choose = expert_ids.shape[1]
    slot_count = saved_routed.shape[2]
    capacity = slot_count // experts
    flat_ids = expert_ids.reshape(-1)
    onehot = (flat_ids[:, None] == jnp.arange(experts, dtype=jnp.int32)[None, :]).astype(jnp.int32)
    earlier = jnp.cumsum(onehot, axis=0) - onehot
    position = jnp.sum(earlier * onehot, axis=1)
    slot_index = flat_ids * capacity + position
    pair_token = jnp.arange(tokens * choose, dtype=jnp.int32) // choose
    source_row = jnp.full((slot_count,), tokens, jnp.int32).at[slot_index].set(pair_token)
    padded = jnp.concatenate([grad_out, jnp.zeros((1, features), grad_out.dtype)], axis=0)
    send_rows = padded[source_row].reshape(experts, capacity, features)
    arrived = lax.all_to_all(send_rows, "expert", split_axis=0, concat_axis=0, tiled=True)
    slot_rows = arrived.reshape(slot_count, features)
    back_grad = contract_last(slot_rows, w_down[0])
    grad_gate, grad_up = swiglu_grads(back_grad, saved_routed[0, 0], saved_routed[0, 1])
    gate_mix = gate_mixture(back_grad, saved_routed[0, 0], saved_routed[0, 1])
    row_terms = contract_last(grad_gate, w_gate_up[0, 0]) + contract_last(grad_up, w_gate_up[0, 1])
    gate_terms = jnp.sum(gate_mix, axis=1).astype(jnp.bfloat16)
    shared_back = contract_last(grad_out, lax.all_gather(shared_down, "expert", axis=1, tiled=True))
    shared_gate, shared_up = swiglu_grads(shared_back, saved_shared[0], saved_shared[1])
    weight_piece = lax.all_gather(shared_gate_up, "expert", axis=1, tiled=True)
    shared_term = contract_last(shared_gate, weight_piece[0]) + contract_last(
        shared_up, weight_piece[1]
    )
    outgoing = row_terms.astype(jnp.bfloat16).reshape(experts, capacity, features)
    returned, gate_back = (
        lax.all_to_all(outgoing, "expert", split_axis=0, concat_axis=0, tiled=True),
        lax.all_to_all(
            gate_terms.reshape(experts, capacity), "expert", split_axis=0, concat_axis=0, tiled=True
        ),
    )
    picked = returned.reshape(slot_count, features)[slot_index].reshape(tokens, choose, features)
    routed = jnp.einsum("tkd,tk->td", picked.astype(jnp.float32), gate_values)
    summed = lax.psum_scatter(
        (routed + shared_term).astype(jnp.bfloat16), "tensor", scatter_dimension=1, tiled=True
    )
    gate_pairs = (
        gate_back.reshape(slot_count)[slot_index].reshape(tokens, choose).astype(jnp.float32)
    )
    grad_gates = lax.psum(gate_pairs, "tensor")
    return (summed, grad_gates)


def solution(mesh):
    return jax.shard_map(
        per_device,
        mesh=mesh,
        in_specs=(
            P("expert", None),
            P("expert", None),
            P("expert", None),
            P("expert", None, None, "tensor"),
            P("expert", "tensor", None),
            P("expert", None, None, "tensor"),
            P(None, "expert", "tensor"),
            P("tensor", "expert"),
            P(None, "expert", "tensor"),
        ),
        out_specs=(P("expert", "tensor"), P("expert", None)),
        check_vma=False,
    )
```

profile of v0, /device:TPU:0, one launch (start us, length us, event | category | flops | bytes accessed | tf_op | source)
XLA Modules:
  0.0 253.5 jit_solution(2283505379111606184)
XLA Ops:
  7.2 0.0 all-gather.3.cloned.1.call-start
  7.2 0.7 all-gather.3.cloned.1.call-update
  7.9 0.0 all-gather.5.cloned.1.call-start
  7.9 0.7 all-gather.5.cloned.1.call-update
  8.6 0.8 copy.18
  9.4 0.1 eq.15
  9.5 0.7 broadcast_multiply_fusion
  10.2 0.1 copy.17
  10.3 0.1 mul.62
  10.4 0.1 fusion.29
  10.4 0.2 reduce_window_sum.11
  10.6 0.9 concatenate.3
  11.5 0.2 select_reduce_fusion
  11.7 1.0 scatter_custom_fusion
  12.7 0.0 copy-start.4
  12.8 1.7 gather_fusion
  14.5 0.0 copy-start.3
  14.5 66.9 %all_to_all.16 = bf16[16,16,3584]{2,1,0:T(8,128)(2,1)S(1)} all-to-all(bf16[16,16,3584]{2,1,0:T(8,128)(2,1)S(1)} %bitcast.73), channel_id=1, replica_groups=mesh['expert'=16,'tensor'=2] {'expert'}, dimensions={0} | all-to-all | bytes 3670016 | tf_op jit(solution)/shard_map/all_to_all | solution.py:56
  81.4 0.0 copy-done.4
  81.4 0.0 copy-done.3
  81.4 0.0 slice-start
  81.4 1.3 fusion.16
  82.7 0.0 slice-start.1
  82.7 3.4 %fusion.5 = f32[256,3584]{1,0:T(8,128)S(1)} fusion(bf16[1,2,3584,512]{3,2,1,0:T(8,128)(2,1)} %param.12, f32[256,512]{1,0:T(8,128)S(1)} %get-tuple-element.9, bf16[1,2,256,512]{3,2,1,0:T(8,128)(2,1)S(1)} %copy-done.4), kind=kOutput, calls=%fused_computation.13 | convolution fusion | flops 941096960 | bytes 8388608 | tf_op jit(solution)/shard_map/dot_general | solution.py:8
  86.2 0.0 slice-done
  86.2 0.0 slice-done.1
  86.2 2.4 fusion
  88.6 0.0 copy-start.2
  88.6 7.1 %all-to-all-start.1 = ((bf16[16,16,3584]{2,1,0:T(8,128)(2,1)}), bf16[16,16,3584]{2,1,0:T(8,128)(2,1)S(1)}, u32[]{:S(2)}, u32[]{:S(2)}) async-start(bf16[16,16,3584]{2,1,0:T(8,128)(2,1)} %bitcast.74), calls=%async_computation.1 | async-start | bytes 3670016 | tf_op jit(solution)/shard_map/all_to_all | solution.py:71
  95.8 0.0 reduce-scatter.2.cloned.1.call-start
  95.8 0.0 copy-done.2
  95.8 0.1 copy.21
  95.9 47.3 %all-to-all-done.1 = bf16[16,16,3584]{2,1,0:T(8,128)(2,1)S(1)} async-done(((bf16[16,16,3584]{2,1,0:T(8,128)(2,1)}), bf16[16,16,3584]{2,1,0:T(8,128)(2,1)S(1)}, u32[]{:S(2)}, u32[]{:S(2)}) %all-to-all-start.1) | async-done | bytes 1835040 | tf_op jit(solution)/shard_map/all_to_all | solution.py:71
  143.2 0.0 copy-start
  143.2 1.1 gather_fusion.1
  144.4 0.0 copy-start.1
  144.4 0.4 fusion.11
  144.8 0.0 all-gather.3.cloned.1.call-done
  144.8 0.0 copy-done
  144.8 2.6 %fusion.56 = f32[16,512]{1,0:T(8,128)S(1)} fusion(bf16[16,3584]{1,0:T(8,128)(2,1)S(1)} %copy-done, bf16[512,3584]{0,1:T(8,128)(2,1)} %all-gather.3.cloned.1.call-done), kind=kOutput, calls=%fused_computation.81 | convolution fusion | flops 58720256 | bytes 3817472 | tf_op jit(solution)/shard_map/dot_general | solution.py:8
  147.4 76.9 %all-gather.5.cloned.1.call-done = bf16[2,3584,512]{2,1,0:T(8,128)(2,1)} async-done(((bf16[2,224,512]{2,1,0:T(8,128)(2,1)}), bf16[2,3584,512]{2,1,0:T(8,128)(2,1)}) %all-gather.5.cloned.1.call-update) | async-done | bytes 7340048 | tf_op jit(solution)/shard_map/all_gather | solution.py:65
  224.3 0.0 copy-done.1
  224.3 3.1 %fusion.3 = f32[16,3584]{1,0:T(8,128)S(1)} fusion(bf16[2,3584,512]{2,1,0:T(8,128)(2,1)} %all-gather.5.cloned.1.call-done, f32[16,512]{1,0:T(8,128)S(1)} %fusion.56, bf16[2,16,512]{2,1,0:T(8,128)(2,1)S(1)} %copy-done.1), kind=kOutput, calls=%fused_computation.11 | convolution fusion | flops 58818560 | bytes 3964928 | tf_op jit(solution)/shard_map/dot_general | solution.py:8
  227.4 3.8 %fusion.2 = bf16[16,3584]{1,0:T(8,128)(2,1)} fusion(f32[16,3584]{1,0:T(8,128)S(1)} %fusion.3, bf16[2,3584,512]{2,1,0:T(8,128)(2,1)} %all-gather.5.cloned.1.call-done, f32[16,1,3584]{2,1,0:T(1,128)S(1)} %fusion.11, f32[16,512]{1,0:T(8,128)S(1)} %fusion.56, bf16[2,16,512]{2,1,0:T(8,128)(2,1)S(1)} %copy-done.1), kind=kOutput, calls=%fused_computation.8 | convolution fusion | flops 58949632 | bytes 4292608 | tf_op jit(solution)/shard_map/dot_general | solution.py:8
  231.2 0.0 reduce-scatter.2.cloned.1.call-update
  231.2 0.1 convert_element_type.92
  231.3 11.1 %all_to_all.17 = bf16[16,1,16]{2,1,0:T(2,128)(2,1)S(1)} all-to-all(bf16[16,1,16]{2,1,0:T(2,128)(2,1)S(1)} %convert_element_type.92), channel_id=1, replica_groups=mesh['expert'=16,'tensor'=2] {'expert'}, dimensions={0} | all-to-all | bytes 1024 | tf_op jit(solution)/shard_map/all_to_all | solution.py:72
  242.4 0.1 reshape.84
  242.5 1.2 gather_fusion.2
  243.7 0.1 reshape.89
  243.8 2.5 psum.7
  246.3 0.7 copy.20
  247.0 0.0 reduce-scatter.2.cloned.1.call-done
  (7 shorter events, 0.1 us)
Async XLA Ops:
  7.2 137.6 %all-gather.3.cloned.1.call-start = ((), (), s32[]{:S(2)}) async-start(), calls=%async_computation.4 | async-start | bytes 3899392 | tf_op jit(solution)/shard_map/all_gather | solution.py:63
  7.9 216.4 %all-gather.5.cloned.1.call-start = ((), (), s32[]{:S(2)}) async-start(), calls=%async_computation.5 | async-start | bytes 7798784 | tf_op jit(solution)/shard_map/all_gather | solution.py:65
  12.7 68.7 %copy-start.4 = (bf16[1,2,256,512]{3,2,1,0:T(8,128)(2,1)S(1)}, bf16[1,2,256,512]{3,2,1,0:T(8,128)(2,1)}, u32[]{:S(2)}) copy-start(bf16[1,2,256,512]{3,2,1,0:T(8,128)(2,1)} %param.14) | copy-start | bytes 1572868
  14.5 66.9 %copy-start.3 = (bf16[1,512,3584]{2,1,0:T(8,128)(2,1)S(1)}, bf16[1,512,3584]{2,1,0:T(8,128)(2,1)}, u32[]{:S(2)}) copy-start(bf16[1,512,3584]{2,1,0:T(8,128)(2,1)} %param.13) | copy-start | bytes 11010052
  81.4 4.8 %slice-start = ((s8[7340032]{0:T(1024)(128)(4,1)}), s8[4194304]{0:T(1024)(128)(4,1)S(1)}, s32[]{:S(2)}) async-start(s8[7340032]{0:T(1024)(128)(4,1)} %bitcast.77), calls=%async_computation.7 | async-start | bytes 8388608
  82.7 3.5 %slice-start.1 = ((s8[7340032]{0:T(1024)(128)(4,1)}), s8[3145728]{0:T(1024)(128)(4,1)S(1)}, s32[]{:S(2)}) async-start(s8[7340032]{0:T(1024)(128)(4,1)} %bitcast.77), calls=%async_computation.8 | async-start | bytes 6291456
  88.6 7.2 %copy-start.2 = (f32[16,8]{0,1:T(8,128)S(1)}, f32[16,8]{0,1:T(8,128)}, u32[]{:S(2)}) copy-start(f32[16,8]{0,1:T(8,128)} %param.11) | copy-start | bytes 1540
  88.6 54.6 %all-to-all-start.1 = ((bf16[16,16,3584]{2,1,0:T(8,128)(2,1)}), bf16[16,16,3584]{2,1,0:T(8,128)(2,1)S(1)}, u32[]{:S(2)}, u32[]{:S(2)}) async-start(bf16[16,16,3584]{2,1,0:T(8,128)(2,1)} %bitcast.74), calls=%async_computation.1 | async-start | bytes 3670016 | tf_op jit(solution)/shard_map/all_to_all | solution.py:71
  95.8 151.2 %reduce-scatter.2.cloned.1.call-start = ((), (), s32[]{:S(2)}) async-start(), calls=%async_computation.6 | async-start | bytes 172032 | tf_op jit(solution)/shard_map/reduce_scatter | solution.py:78
  143.2 1.6 copy-start
  144.4 79.9 %copy-start.1 = (bf16[2,16,512]{2,1,0:T(8,128)(2,1)S(1)}, bf16[2,16,512]{2,1,0:T(8,128)(2,1)}, u32[]{:S(2)}) copy-start(bf16[2,16,512]{2,1,0:T(8,128)(2,1)} %param.17) | copy-start | bytes 98308
Sparse Core Ops, SparseCore 0:
  10.7 103.8 all-gather.2
  117.3 106.9 all-gather.4
  231.3 5.9 reduce-scatter.1
where the time goes:
time: 254 us; the launch traced here: 253 us
  waiting for transfers between devices  126 us (50%)
  blocking collectives  80.5 us (32%)
  matrix products  17 us (7%)
  between operations  13.9 us (5%)
  local copies, waits for them, and re-layouts  8 us (3%)
  starting transfers between devices  7.26 us (3%)
    all_gather x1, waiting for transfers between devices, per_device(): weight_piece = lax.all_gather(shared_gate_up, 'expert', axis=1, tiled=True)  76.9 us
    all_to_all x1, blocking collectives, per_device(): lax.all_to_all(send_rows, 'expert', split_axis=0, concat_axis=0, tiled=True)  66.9 us
    all_to_all x1, waiting for transfers between devices, per_device(): lax.all_to_all(outgoing, 'expert', split_axis=0, concat_axis=0, tiled=True)  47.3 us
    dot_general x6, matrix products, contract_last(): lax.dot_general(left_side, right_side, (((1,), (1,)), ((), ())), preferre...  16.7 us
    all_to_all x1, blocking collectives, per_device(): lax.all_to_all(gate_terms.reshape(experts, capacity), 'expert', split_axi...  11.1 us
    all_to_all x1, starting transfers between devices, per_device(): lax.all_to_all(outgoing, 'expert', split_axis=0, concat_axis=0, tiled=True)  7.14 us
  transfers between devices with their start and end apart: 4, of which 2 were waited for; matrix products, arithmetic and copies ran while one was open for 8% of the time, Pallas kernels for 0%

commit v1 on v0

v1 whole, which is shorter than its diff:
```python
import functools

import jax
import jax.numpy as jnp
from jax import lax
from jax.experimental import pallas as pl
from jax.experimental.pallas import tpu as pltpu
from jax.sharding import PartitionSpec as P

MESH = pl.DeviceIdType.MESH
LANES = 128


def dot_nt(left, right):
    return lax.dot_general(
        left, right, (((1,), (1,)), ((), ())), preferred_element_type=jnp.float32
    )


def loop(count, body):
    def step(i, carry):
        body(i)
        return carry

    lax.fori_loop(0, count, step, 0)


def flat(value):
    return value.reshape(-1, value.shape[-1])


def kernel(
    E, T, F, NC, TOP,
    g_ref, x_ref, m_ref, sv_ref, sgu_ref, sd_ref, wd_hbm, wgu_hbm, sr_hbm,
    out_r, out_s, out_g,
    gbuf, xbuf, mbuf, wd, wgu, sr,
    ps, s2buf, s3buf, st, s4buf, s4pair, gm, gmbuf, gpair,
    pairsend, pairbuf, part, r3buf, r2buf, rzbuf,
    wsem, g_recv, g_sz, g_s2, g_s3, g_ps, g_pr,
    s3_recv, s3_sz, s3_s2, s3_s3,
    x_s, x_r, m_s, m_r, s2_s, s2_r, s4_s, s4_r, gm_s, gm_r,
    s4p_s, s4p_r, gp_s, gp_r, pair_s, pair_r,
    r3_s, r3_r, r2_s, r2_r, rz_s, rz_r,
):
    me = lax.axis_index("expert")
    j = lax.axis_index("tensor")
    A = E // 4
    a = me // 4
    r = me % 4
    rc = r + 1 - 2 * (r % 2)
    rb = r + 2 - 4 * (r // 2)
    odd = j % 2
    r2 = rc * (1 - odd) + rb * odd
    r3 = rb * (1 - odd) + rc * odd
    r23 = 3 - r
    p2 = a * 4 + r2
    p3 = a * 4 + r3
    fj = j if F > 1 else 0
    tok = x_ref.shape[1]
    FFl = wd.shape[0]
    H = g_ref.shape[2]
    HR = part.shape[3] * NC
    HC = part.shape[3]
    tokens = E * tok

    def rc_(src, dst, ssem, rsem, chip, core):
        return pltpu.make_async_remote_copy(
            src_ref=src, dst_ref=dst, send_sem=ssem, recv_sem=rsem,
            device_id=(chip, core), device_id_type=MESH,
        )

    wcopies = [
        pltpu.make_async_copy(sr_hbm, sr, wsem.at[0]),
        pltpu.make_async_copy(wd_hbm, wd, wsem.at[1]),
        pltpu.make_async_copy(wgu_hbm, wgu, wsem.at[2]),
    ]
    for copy in wcopies:
        copy.start()

    barrier = pltpu.get_barrier_semaphore()

    def greet(i):
        pl.semaphore_signal(barrier, inc=1, device_id=((me + i + 1) % E, j), device_id_type=MESH)

    loop(E - 1, greet)
    for d in range(1, T):
        pl.semaphore_signal(barrier, inc=1, device_id=(me, (j + d) % T), device_id_type=MESH)
    pl.semaphore_wait(barrier, E - 1 + T - 1)

    def a2a_send(src_of, dst, ssem, rsem):
        def body(i):
            o = (me + i + 1) % E
            rc_(src_of(o), dst.at[me], ssem.at[o], rsem.at[me], o, j).start()

        loop(E - 1, body)

    def a2a_wait(dst, rsem):
        def body(i):
            o = (me + i + 1) % E
            rc_(dst.at[o], dst.at[o], rsem.at[o], rsem.at[o], o, j).wait_recv()

        loop(E - 1, body)

    def a2a_drain(src_of, ssem):
        def body(i):
            o = (me + i + 1) % E
            rc_(src_of(o), src_of(o), ssem.at[o], ssem.at[o], o, j).wait_send()

        loop(E - 1, body)

    class Tree:
        def __init__(self, buf, own, recv, sz, s2, s3, hook):
            self.buf, self.own, self.recv = buf, own, recv
            self.sz, self.s2, self.s3, self.hook = sz, s2, s3, hook

        def send(self, blk, ssem, chip, src=None):
            src = self.buf.at[blk] if src is None else src
            rc_(src, self.buf.at[blk], ssem, self.recv.at[blk], chip, j).start()

        def wait(self, blk):
            rc_(self.buf.at[blk], self.buf.at[blk], self.recv.at[blk], self.recv.at[blk], p2, j).wait_recv()

        def start(self):
            self.send(me, self.s3.at[0], p3, self.own)
            self.send(me, self.s2.at[0], p2, self.own)

            def body(i):
                self.send(me, self.sz.at[i], ((a + i + 1) % A) * 4 + r, self.own)

            loop(A - 1, body)
            self.hook(me, self.own)

        def stage_z(self):
            def body(i):
                blk = ((a + i + 1) % A) * 4 + r
                self.wait(blk)
                self.send(blk, self.s3.at[i + 1], p3)
                self.send(blk, self.s2.at[i + 1], p2)
                self.hook(blk, self.buf.at[blk])

            loop(A - 1, body)

        def stage_2(self):
            def body(i):
                blk = ((a + i) % A) * 4 + r2
                self.wait(blk)
                self.send(blk, self.s3.at[A + i], p3)
                self.hook(blk, self.buf.at[blk])

            loop(A, body)

        def stage_3(self):
            for rr in (r3, r23):
                def body(i):
                    blk = ((a + i) % A) * 4 + rr
                    self.wait(blk)
                    self.hook(blk, self.buf.at[blk])

                loop(A, body)

        def drain(self):
            def one(sem):
                rc_(self.own, self.own, sem, sem, p2, j).wait_send()

            loop(A - 1, lambda i: one(self.sz.at[i]))
            loop(A, lambda i: one(self.s2.at[i]))
            loop(2 * A, lambda i: one(self.s3.at[i]))

    def pair_hook(blk, src):
        if F > 1:
            for d in range(1, T):
                rc_(
                    src, gbuf.at[j, blk], g_ps.at[d, blk], g_pr.at[j, blk], me, (j + d) % T
                ).start()

    tree_g = Tree(gbuf.at[fj], g_ref.at[fj], g_recv, g_sz, g_s2, g_s3, pair_hook)
    tree_s = Tree(s3buf, s3buf.at[me], s3_recv, s3_sz, s3_s2, s3_s3, lambda blk, src: None)

    a2a_send(lambda o: x_ref.at[o], xbuf, x_s, x_r)
    tree_g.start()
    a2a_send(lambda o: m_ref, mbuf, m_s, m_r)
    xbuf[me] = x_ref[me]
    mbuf[me] = m_ref[...]
    gbuf[fj, me] = g_ref[fj]

    a2a_wait(xbuf, x_r)
    ps[...] = dot_nt(flat(xbuf[...]), sd_ref[...]).astype(jnp.bfloat16).reshape(E, tok, FFl)
    a2a_send(lambda o: ps.at[o], s2buf, s2_s, s2_r)
    s2buf[me] = ps[me]

    tree_g.stage_z()

    a2a_wait(mbuf, m_r)
    meta = flat(mbuf[...])
    lane = lax.broadcasted_iota(jnp.int32, (tokens, LANES), 1)
    hit = jnp.where((meta == me.astype(jnp.float32)) & (lane < TOP), 1.0, 0.0)
    gates = pltpu.roll(meta, LANES - TOP, 1)
    chosen = jnp.sum(hit, axis=1, keepdims=True)
    gate = jnp.sum(hit * gates, axis=1, keepdims=True)
    wide = jnp.broadcast_to(chosen, (tokens, LANES))
    row = lax.broadcasted_iota(jnp.int32, (tokens, LANES), 0) % tok
    total = wide
    shift = 1
    while shift < tok:
        total = total + jnp.where(row >= shift, pltpu.roll(total, shift, 0), 0.0)
        shift *= 2
    position = (total - wide)[:, :1]
    slots = sr.shape[1]
    cap = slots // E
    base = (lax.broadcasted_iota(jnp.int32, (tokens, 1), 0) // tok) * cap
    target = position + base.astype(jnp.float32)
    slot = lax.broadcasted_iota(jnp.int32, (tokens, slots), 1).astype(jnp.float32)
    permute = jnp.where((slot == target) & (chosen > 0.5), 1.0, 0.0).astype(jnp.bfloat16)

    tree_g.stage_2()

    wcopies[0].wait()
    pre_gate = jnp.dot(permute, sr[0], preferred_element_type=jnp.float32)
    pre_up = jnp.dot(permute, sr[1], preferred_element_type=jnp.float32)
    sig = jax.nn.sigmoid(pre_gate)
    d_up = pre_gate * sig
    d_gate = pre_up * sig * (1.0 + pre_gate * (1.0 - sig))

    a2a_wait(s2buf, s2_r)
    shared_back = jnp.sum(s2buf[...].astype(jnp.float32), axis=0)
    sh = sv_ref[0].astype(jnp.float32)
    su = sv_ref[1].astype(jnp.float32)
    ssig = jax.nn.sigmoid(sh)
    s3buf[me, 0] = (shared_back * su * ssig * (1.0 + sh * (1.0 - ssig))).astype(jnp.bfloat16)
    s3buf[me, 1] = (shared_back * sh * ssig).astype(jnp.bfloat16)
    tree_s.start()

    tree_g.stage_3()
    tree_s.stage_z()

    wcopies[1].wait()
    if F > 1:
        back = jnp.zeros((tokens, FFl), jnp.float32)
        for d in range(1, T):
            other = (j + d) % T

            def body(i):
                ref = gbuf.at[other, i]
                rc_(ref, ref, g_pr.at[other, i], g_pr.at[other, i], me, other).wait_recv()

            loop(E, body)
        for t in range(F):
            back = back + dot_nt(flat(gbuf[t]), wd[:, t * H:(t + 1) * H])
    else:
        back = dot_nt(flat(gbuf[0]), wd[...])
    tree_s.stage_2()
    grad_up = back * d_up
    gate_sum = jnp.sum(grad_up * pre_up, axis=1, keepdims=True)
    gate_sum = gate_sum.astype(jnp.bfloat16).astype(jnp.float32)
    grad_gate = (back * d_gate * gate).astype(jnp.bfloat16)
    grad_up = (grad_up * gate).astype(jnp.bfloat16)
    gm[...] = jnp.where(lane == me, gate_sum, 0.0).reshape(E, tok, LANES)
    a2a_send(lambda o: gm.at[o], gmbuf, gm_s, gm_r)
    gmbuf[me] = gm[me]

    wcopies[2].wait()

    def rows_of(t, c):
        span = pl.ds(pl.multiple_of(t * HR + c * HC, 16), HC)
        return dot_nt(grad_gate, wgu[0, span, :]) + dot_nt(grad_up, wgu[1, span, :])

    for c in range(NC):
        for d in range(1, T):
            t = (j + d) % T
            pairsend[d - 1, c] = rows_of(t, c).astype(jnp.bfloat16)
            rc_(
                pairsend.at[d - 1, c], pairbuf.at[T - 1 - d, c],
                pair_s.at[d - 1, c], pair_r.at[T - 1 - d, c], me, t,
            ).start()

    def stage3_blocks(c, i):
        ap = i // 2
        w = i % 2
        blk = ap * 4 + r3 * (1 - w) + r23 * w
        return rc_(part.at[c, blk], r3buf.at[c, i], r3_s.at[c, i], r3_r.at[c, i], p3, j)

    for c in range(NC):
        mine = rows_of(j, c)
        for d in range(1, T):
            rc_(
                pairsend.at[d - 1, c], pairbuf.at[d - 1, c],
                pair_s.at[d - 1, c], pair_r.at[d - 1, c], me, (j + d) % T,
            ).wait_recv()
            mine = mine + pairbuf[d - 1, c].astype(jnp.float32)
        part[c] = mine.astype(jnp.bfloat16).reshape(E, tok, HC)
        loop(2 * A, lambda i: stage3_blocks(c, i).start())

    tree_s.stage_3()
    term = dot_nt(flat(s3buf[:, 0]), sgu_ref[0]) + dot_nt(flat(s3buf[:, 1]), sgu_ref[1])
    st[...] = term.astype(jnp.bfloat16).reshape(E, tok, st.shape[2])
    a2a_send(lambda o: st.at[o], s4buf, s4_s, s4_r)
    s4buf[me] = st[me]

    def stage2_block(c, i):
        return rc_(part.at[c, i * 4 + r2], r2buf.at[c, i], r2_s.at[c, i], r2_r.at[c, i], p2, j)

    for c in range(NC):
        loop(2 * A, lambda i: stage3_blocks(c, i).wait_recv())

        def add_first(i):
            blk = i * 4 + r2
            part[c, blk] = (
                part[c, blk].astype(jnp.float32) + r3buf[c, i * 2 + 1].astype(jnp.float32)
            ).astype(jnp.bfloat16)

        loop(A, add_first)
        loop(A, lambda i: stage2_block(c, i).start())

    def stagez_block(c, i):
        o = (a + i + 1) % A
        return rc_(
            part.at[c, o * 4 + r], rzbuf.at[c, a], rz_s.at[c, o], rz_r.at[c, a], o * 4 + r, j
        )

    for c in range(NC):
        loop(A, lambda i: stage2_block(c, i).wait_recv())

        def add_second(i):
            blk = i * 4 + r
            part[c, blk] = (
                part[c, blk].astype(jnp.float32)
                + r3buf[c, i * 2].astype(jnp.float32)
                + r2buf[c, i].astype(jnp.float32)
            ).astype(jnp.bfloat16)

        loop(A, add_second)
        loop(A - 1, lambda i: stagez_block(c, i).start())
        rzbuf[c, a] = part[c, me]

    a2a_wait(gmbuf, gm_r)
    gpair[T - 1] = jnp.sum(gmbuf[...], axis=0)
    a2a_wait(s4buf, s4_r)
    group = E // T
    for d in range(1, T):
        t = (j + d) % T
        rc_(gpair.at[T - 1], gpair.at[T - 1 - d], gp_s.at[d - 1], gp_r.at[T - 1 - d], me, t).start()
        rc_(
            s4buf.at[pl.ds(t * group, group)], s4pair.at[T - 1 - d],
            s4p_s.at[d - 1], s4p_r.at[T - 1 - d], me, t,
        ).start()
    shared = s4buf[pl.ds(j * group, group)].astype(jnp.float32)
    for d in range(1, T):
        rc_(gpair.at[T - 1], gpair.at[d - 1], gp_s.at[d - 1], gp_r.at[d - 1], me, (j + d) % T).wait_recv()
        rc_(
            s4pair.at[d - 1], s4pair.at[d - 1], s4p_s.at[d - 1], s4p_r.at[d - 1], me, (j + d) % T
        ).wait_recv()
        shared = shared + s4pair[d - 1].astype(jnp.float32)
    out_s[...] = shared
    sums = jnp.sum(gpair[...], axis=0)
    own_meta = m_ref[...]
    lane16 = lax.broadcasted_iota(jnp.int32, (tok, LANES), 1)
    lane_f = lane16.astype(jnp.float32)
    result = jnp.zeros((tok, LANES), jnp.float32)
    for k in range(TOP):
        value = jnp.sum(
            jnp.where(lane_f == own_meta[:, k:k + 1], sums, 0.0), axis=1, keepdims=True
        )
        result = jnp.where(lane16 == k, value, result)
    out_g[...] = result

    for c in range(NC):
        def wait_z(i):
            o = (a + i + 1) % A
            rc_(rzbuf.at[c, o], rzbuf.at[c, o], rz_s.at[c, o], rz_r.at[c, o], p2, j).wait_recv()

        loop(A - 1, wait_z)
        out_r[c] = jnp.sum(rzbuf[c].astype(jnp.float32), axis=0)

    a2a_drain(lambda o: x_ref.at[o], x_s)
    a2a_drain(lambda o: m_ref, m_s)
    a2a_drain(lambda o: ps.at[o], s2_s)
    a2a_drain(lambda o: gm.at[o], gm_s)
    a2a_drain(lambda o: st.at[o], s4_s)
    tree_g.drain()
    tree_s.drain()
    for d in range(1, T):
        if F > 1:
            loop(
                E,
                lambda i: rc_(
                    gbuf.at[j, i], gbuf.at[j, i], g_ps.at[d, i], g_ps.at[d, i], me, (j + d) % T
                ).wait_send(),
            )
        rc_(gpair.at[T - 1], gpair.at[T - 1], gp_s.at[d - 1], gp_s.at[d - 1], me, (j + d) % T).wait_send()
        rc_(
            s4pair.at[d - 1], s4pair.at[d - 1], s4p_s.at[d - 1], s4p_s.at[d - 1], me, (j + d) % T
        ).wait_send()
        for c in range(NC):
            ref = pairsend.at[d - 1, c]
            rc_(ref, ref, pair_s.at[d - 1, c], pair_s.at[d - 1, c], me, (j + d) % T).wait_send()
    for c in range(NC):
        loop(2 * A, lambda i: stage3_blocks(c, i).wait_send())
        loop(A, lambda i: stage2_block(c, i).wait_send())
        loop(A - 1, lambda i: stagez_block(c, i).wait_send())


def per_device(
    E, T,
    grad_out, expert_ids, gate_values, w_gate_up, w_down, saved_routed,
    shared_gate_up, shared_down, saved_shared,
):
    tok, D = grad_out.shape
    TOP = expert_ids.shape[1]
    FFl = w_down.shape[1]
    DS = shared_down.shape[1]
    slots = saved_routed.shape[2]
    F = T if (D // T) % LANES == 0 else 1
    H = D // F
    HR = D // T
    NC = 2 if HR % (2 * LANES) == 0 else 1
    HC = HR // NC
    A = E // 4
    tokens = E * tok
    halves = grad_out.reshape(tok, F, H).transpose(1, 0, 2)
    pieces = grad_out.reshape(tok, E, DS).transpose(1, 0, 2)
    meta = jnp.concatenate(
        [
            expert_ids.astype(jnp.float32),
            gate_values,
            jnp.zeros((tok, LANES - 2 * TOP), jnp.float32),
        ],
        axis=1,
    )
    bf, f32 = jnp.bfloat16, jnp.float32
    V, S = pltpu.VMEM, pltpu.SemaphoreType.DMA
    T1 = max(T - 1, 1)
    scratch = [
        V((F, E, tok, H), bf), V((E, tok, DS), bf), V((E, tok, LANES), f32),
        V((FFl, D), bf), V((2, D, FFl), bf), V((2, slots, FFl), bf),
        V((E, tok, FFl), bf), V((E, tok, FFl), bf), V((E, 2, tok, FFl), bf),
        V((E, tok, DS), bf), V((E, tok, DS), bf), V((T1, E // T, tok, DS), bf),
        V((E, tok, LANES), f32), V((E, tok, LANES), f32), V((T, tok, LANES), f32),
        V((T1, NC, tokens, HC), bf), V((T1, NC, tokens, HC), bf), V((NC, E, tok, HC), bf),
        V((NC, 2 * A, tok, HC), bf), V((NC, A, tok, HC), bf), V((NC, A, tok, HC), bf),
        S((3,)), S((E,)), S((A,)), S((A,)), S((2 * A,)), S((T, E)), S((T, E)),
        S((E,)), S((A,)), S((A,)), S((2 * A,)),
        S((E,)), S((E,)), S((E,)), S((E,)), S((E,)), S((E,)), S((E,)), S((E,)), S((E,)), S((E,)),
        S((T1,)), S((T1,)), S((T1,)), S((T1,)), S((T1, NC)), S((T1, NC)),
        S((NC, 2 * A)), S((NC, 2 * A)), S((NC, A)), S((NC, A)), S((NC, A)), S((NC, A)),
    ]
    vm = pl.BlockSpec(memory_space=pltpu.VMEM)
    hbm = pl.BlockSpec(memory_space=pltpu.HBM)
    routed, shared, gates = pl.pallas_call(
        functools.partial(kernel, E, T, F, NC, TOP),
        out_shape=(
            jax.ShapeDtypeStruct((NC, tok, HC), f32),
            jax.ShapeDtypeStruct((E // T, tok, DS), f32),
            jax.ShapeDtypeStruct((tok, LANES), f32),
        ),
        in_specs=[vm] * 6 + [hbm] * 3,
        out_specs=(vm, vm, vm),
        scratch_shapes=scratch,
        compiler_params=pltpu.CompilerParams(
            collective_id=0, has_side_effects=True, vmem_limit_bytes=60 * 1024 * 1024
        ),
    )(
        halves, pieces, meta, saved_shared, shared_gate_up, shared_down,
        w_down[0], w_gate_up[0], saved_routed[0],
    )
    routed = routed.transpose(1, 0, 2).reshape(tok, HR)
    shared = shared.transpose(1, 0, 2).reshape(tok, HR)
    return (routed + shared).astype(bf), gates[:, :TOP]


def solution(mesh):
    return jax.shard_map(
        functools.partial(per_device, mesh.shape["expert"], mesh.shape["tensor"]),
        mesh=mesh,
        in_specs=(
            P("expert", None),
            P("expert", None),
            P("expert", None),
            P("expert", None, None, "tensor"),
            P("expert", "tensor", None),
            P("expert", None, None, "tensor"),
            P(None, "expert", "tensor"),
            P("tensor", "expert"),
            P(None, "expert", "tensor"),
        ),
        out_specs=(P("expert", "tensor"), P("expert", None)),
        check_vma=False,
    )
```

time: 254 us -> 73.2 us (0.29)
  waiting for transfers between devices: 126 us -> 0 us
  blocking collectives: 80.5 us -> 0 us
  Pallas kernels: 0 us -> 60.8 us
  matrix products: 17 us -> 0 us
  between operations: 13.9 us -> 0.66 us
  starting transfers between devices: 7.26 us -> 0 us
    all_to_all x2 -> x0, blocking collectives: 78 us -> none  [the longest x1 66.9 us: per_device(): lax.all_to_all(send_rows, 'expert', split_axis=0, concat_axis=0, tiled=True)]
    all_gather x2 -> x0, waiting for transfers between devices: 76.9 us -> none  [the longest x1 76.9 us: per_device(): weight_piece = lax.all_gather(shared_gate_up, 'expert', axis=1, tiled=True)]
    pallas_call x0 -> x1, Pallas kernels: none -> 60.8 us  [per_device(): pl.pallas_call(functools.partial(kernel, E, T, F, NC, TOP), out_shape=(ja...]
    all_to_all x1 -> x0, waiting for transfers between devices: 47.3 us -> none  [per_device(): lax.all_to_all(outgoing, 'expert', split_axis=0, concat_axis=0, tiled=True)]
    dot_general x7 -> x0, matrix products: 17 us -> none  [the longest x6 16.7 us: contract_last(): lax.dot_general(left_side, right_side, (((1,), (1,)), ((), ())), preferre...]
    all_to_all x1 -> x0, starting transfers between devices: 7.14 us -> none  [per_device(): lax.all_to_all(outgoing, 'expert', split_axis=0, concat_axis=0, tiled=True)]
    reshape x1 -> x5, local copies, waits for them, and re-layouts: 0.09 us -> 4.36 us  [the longest x2 1.8 us: per_device(): pieces = grad_out.reshape(tok, E, DS).transpose(1, 0, 2)]
    gather x3 -> x0, local copies, waits for them, and re-layouts: 4.07 us -> none  [the longest x1 1.72 us: per_device(): send_rows = padded[source_row].reshape(experts, capacity, features)]
  transfers between devices with their start and end apart: 4 -> 0, of which waited for: 2 -> 0; matrix products, arithmetic and copies ran while one was open for 8% -> 0% of each run, Pallas kernels for 0% -> 0%
where the time goes in v1:
time: 73.2 us; the launch traced here: 72.9 us
  Pallas kernels  60.8 us (83%)
  local copies, waits for them, and re-layouts  9.38 us (13%)
  other arithmetic  2 us (3%)
    pallas_call x1, Pallas kernels, per_device(): pl.pallas_call(functools.partial(kernel, E, T, F, NC, TOP), out_shape=(ja...  60.8 us
    unnamed x3, local copies, waits for them, and re-layouts  3.88 us
    reshape x2, local copies, waits for them, and re-layouts, per_device(): pieces = grad_out.reshape(tok, E, DS).transpose(1, 0, 2)  1.8 us
    reshape x1, local copies, waits for them, and re-layouts, per_device(): halves = grad_out.reshape(tok, F, H).transpose(1, 0, 2)  1.55 us

profile of v1, /device:TPU:0, one launch (start us, length us, event | category | flops | bytes accessed | tf_op | source)
XLA Modules:
  0.0 72.9 jit_solution(4445373163644668498)
XLA Ops:
  0.6 0.1 pad.2.clone
  0.7 0.7 convert_element_type.6
  1.4 0.1 copy.25
  1.5 0.8 %copy.26 = f32[16,8]{1,0:T(8,128)S(1)} copy(f32[16,8]{0,1:T(8,128)} %param.11) | data formatting | bytes 1024 | tf_op args[2]
  2.2 0.7 maximum_maximum_fusion.m_ref
  2.9 1.6 %copy.36 = bf16[2,2,8,1792]{3,2,0,1:T(8,128)(2,1)} copy(bf16[2,2,8,1792]{3,2,1,0:T(8,128)(2,1)} %bitcast.24) | data formatting | bytes 229376 | tf_op jit(solution)/shard_map/reshape | solution.py:419
  4.5 1.1 %reshape.17 = bf16[16,16,224]{2,1,0:T(8,128)(2,1)S(1)} reshape(bf16[16,3584]{1,0:T(8,128)(2,1)} %param.9) | data formatting | bytes 229376 | tf_op jit(solution)/shard_map/reshape | solution.py:420
  5.6 0.7 copy.35
  6.3 1.8 %copy.27.sd_ref = bf16[512,224]{1,0:T(8,128)(2,1)} copy(bf16[512,224]{0,1:T(8,128)(2,1)} %param.16) | data formatting | bytes 458752 | tf_op args[7]
  8.0 60.8 %shard_map.104 = (f32[2,16,896]{2,1,0:T(8,128)}, f32[8,16,224]{2,1,0:T(8,128)}, f32[16,128]{1,0:T(8,128)}) custom-call(bf16[2,16,1792]{2,1,0:T(8,128)(2,1)} %bitcast.22, bf16[16,16,224]{2,1,0:T(8,128)(2,1)} %bitcast.20, f32[16,128]{1,0:T(8,128)} %maximum_maximum_fusion.m_ref, bf16[2,16,512]{2,1,0:T(8,128)(2,1)} %sv_ref.1, bf16[2,224,512]{2,1,0:T(8,128)(2,1)} %sgu_ref.1, ...), custom_call_target="tpu_custom_call" | custom-call | tf_op jit(solution)/shard_map/pallas_call | solution.py:448
  68.9 0.9 %copy.32 = f32[2,2,8,896]{3,2,0,1:T(8,128)S(1)} copy(f32[2,2,8,896]{3,2,1,0:T(8,128)} %bitcast.26) | data formatting | bytes 229376 | tf_op jit(solution)/shard_map/reshape | solution.py:465
  69.8 1.0 %copy.29 = f32[16,8,224]{2,1,0:T(8,128)S(1)} copy(f32[16,8,224]{2,0,1:T(8,128)} %bitcast.25) | data formatting | bytes 229376 | tf_op jit(solution)/shard_map/transpose | solution.py:466
  70.8 0.1 reshape.19
  70.9 0.6 add_convert_fusion
  71.5 1.4 %copy.30 = f32[16,8]{0,1:T(8,128)} copy(f32[16,8]{1,0:T(8,128)} %bitcast.27) | data formatting | bytes 1024
  (1 shorter events, 0.0 us)

commit v2 on v1

--- a/solution.py
+++ b/solution.py
@@ -31,9 +31,9 @@
 
 def kernel(
     E, T, F, NC, TOP,
-    g_ref, x_ref, m_ref, sv_ref, sgu_ref, sd_ref, wd_hbm, wgu_hbm, sr_hbm,
-    out_r, out_s, out_g,
-    gbuf, xbuf, mbuf, wd, wgu, sr,
+    g_ref, id_ref, gv_ref, sv_ref, sgu_ref, sd_ref, wd_hbm, wgu_hbm, sr_hbm,
+    out_r, out_g,
+    x_ref, m_ref, square, spread, gbuf, xbuf, mbuf, wd, wgu, sr,
     ps, s2buf, s3buf, st, s4buf, s4pair, gm, gmbuf, gpair,
     pairsend, pairbuf, part, r3buf, r2buf, rzbuf,
     wsem, g_recv, g_sz, g_s2, g_s3, g_ps, g_pr,
@@ -57,8 +57,10 @@
     p3 = a * 4 + r3
     fj = j if F > 1 else 0
     tok = x_ref.shape[1]
+    DS = x_ref.shape[2]
     FFl = wd.shape[0]
-    H = g_ref.shape[2]
+    H = gbuf.shape[3]
+    own_g = g_ref.at[:, pl.ds(pl.multiple_of(fj * H, LANES), H)] if F > 1 else g_ref
     HR = part.shape[3] * NC
     HC = part.shape[3]
     tokens = E * tok
@@ -85,6 +87,14 @@
     loop(E - 1, greet)
     for d in range(1, T):
         pl.semaphore_signal(barrier, inc=1, device_id=(me, (j + d) % T), device_id_type=MESH)
+
+    for o in range(E):
+        x_ref[o] = g_ref[:, o * DS:(o + 1) * DS]
+    square[...] = jnp.zeros_like(square)
+    square[0:TOP, 0:tok] = id_ref[...].astype(jnp.float32)
+    square[TOP:2 * TOP, 0:tok] = gv_ref[...]
+    m_ref[...] = square[...].T[0:tok]
+
     pl.semaphore_wait(barrier, E - 1 + T - 1)
 
     def a2a_send(src_of, dst, ssem, rsem):
@@ -173,7 +183,7 @@
                     src, gbuf.at[j, blk], g_ps.at[d, blk], g_pr.at[j, blk], me, (j + d) % T
                 ).start()
 
-    tree_g = Tree(gbuf.at[fj], g_ref.at[fj], g_recv, g_sz, g_s2, g_s3, pair_hook)
+    tree_g = Tree(gbuf.at[fj], own_g, g_recv, g_sz, g_s2, g_s3, pair_hook)
     tree_s = Tree(s3buf, s3buf.at[me], s3_recv, s3_sz, s3_s2, s3_s3, lambda blk, src: None)
 
     a2a_send(lambda o: x_ref.at[o], xbuf, x_s, x_r)
@@ -181,10 +191,10 @@
     a2a_send(lambda o: m_ref, mbuf, m_s, m_r)
     xbuf[me] = x_ref[me]
     mbuf[me] = m_ref[...]
-    gbuf[fj, me] = g_ref[fj]
+    gbuf[fj, me] = own_g[...]
 
     a2a_wait(xbuf, x_r)
-    ps[...] = dot_nt(flat(xbuf[...]), sd_ref[...]).astype(jnp.bfloat16).reshape(E, tok, FFl)
+    ps[...] = jnp.dot(flat(xbuf[...]), sd_ref[...], preferred_element_type=jnp.float32).astype(jnp.bfloat16).reshape(E, tok, FFl)
     a2a_send(lambda o: ps.at[o], s2buf, s2_s, s2_r)
     s2buf[me] = ps[me]
 
@@ -350,7 +360,8 @@
             s4pair.at[d - 1], s4pair.at[d - 1], s4p_s.at[d - 1], s4p_r.at[d - 1], me, (j + d) % T
         ).wait_recv()
         shared = shared + s4pair[d - 1].astype(jnp.float32)
-    out_s[...] = shared
+    for o in range(group):
+        spread[:, o * DS:(o + 1) * DS] = shared[o]
     sums = jnp.sum(gpair[...], axis=0)
     own_meta = m_ref[...]
     lane16 = lax.broadcasted_iota(jnp.int32, (tok, LANES), 1)
@@ -361,7 +372,8 @@
             jnp.where(lane_f == own_meta[:, k:k + 1], sums, 0.0), axis=1, keepdims=True
         )
         result = jnp.where(lane16 == k, value, result)
-    out_g[...] = result
+    square[0:tok] = result
+    out_g[...] = square[...].T[0:TOP, 0:tok]
 
     for c in range(NC):
         def wait_z(i):
@@ -369,7 +381,10 @@
             rc_(rzbuf.at[c, o], rzbuf.at[c, o], rz_s.at[c, o], rz_r.at[c, o], p2, j).wait_recv()
 
         loop(A - 1, wait_z)
-        out_r[c] = jnp.sum(rzbuf[c].astype(jnp.float32), axis=0)
+        span = slice(c * HC, (c + 1) * HC)
+        out_r[:, span] = (
+            jnp.sum(rzbuf[c].astype(jnp.float32), axis=0) + spread[:, span]
+        ).astype(jnp.bfloat16)
 
     a2a_drain(lambda o: x_ref.at[o], x_s)
     a2a_drain(lambda o: m_ref, m_s)
@@ -416,20 +431,11 @@
     HC = HR // NC
     A = E // 4
     tokens = E * tok
-    halves = grad_out.reshape(tok, F, H).transpose(1, 0, 2)
-    pieces = grad_out.reshape(tok, E, DS).transpose(1, 0, 2)
-    meta = jnp.concatenate(
-        [
-            expert_ids.astype(jnp.float32),
-            gate_values,
-            jnp.zeros((tok, LANES - 2 * TOP), jnp.float32),
-        ],
-        axis=1,
-    )
     bf, f32 = jnp.bfloat16, jnp.float32
     V, S = pltpu.VMEM, pltpu.SemaphoreType.DMA
     T1 = max(T - 1, 1)
     scratch = [
+        V((E, tok, DS), bf), V((tok, LANES), f32), V((LANES, LANES), f32), V((tok, HR), f32),
         V((F, E, tok, H), bf), V((E, tok, DS), bf), V((E, tok, LANES), f32),
         V((FFl, D), bf), V((2, D, FFl), bf), V((2, slots, FFl), bf),
         V((E, tok, FFl), bf), V((E, tok, FFl), bf), V((E, 2, tok, FFl), bf),
@@ -445,26 +451,23 @@
     ]
     vm = pl.BlockSpec(memory_space=pltpu.VMEM)
     hbm = pl.BlockSpec(memory_space=pltpu.HBM)
-    routed, shared, gates = pl.pallas_call(
+    grad_in, gates = pl.pallas_call(
         functools.partial(kernel, E, T, F, NC, TOP),
         out_shape=(
-            jax.ShapeDtypeStruct((NC, tok, HC), f32),
-            jax.ShapeDtypeStruct((E // T, tok, DS), f32),
-            jax.ShapeDtypeStruct((tok, LANES), f32),
+            jax.ShapeDtypeStruct((tok, HR), bf),
+            jax.ShapeDtypeStruct((TOP, tok), f32),
         ),
         in_specs=[vm] * 6 + [hbm] * 3,
-        out_specs=(vm, vm, vm),
+        out_specs=(vm, vm),
         scratch_shapes=scratch,
         compiler_params=pltpu.CompilerParams(
             collective_id=0, has_side_effects=True, vmem_limit_bytes=60 * 1024 * 1024
         ),
     )(
-        halves, pieces, meta, saved_shared, shared_gate_up, shared_down,
+        grad_out, expert_ids.T, gate_values.T, saved_shared, shared_gate_up, shared_down.T,
         w_down[0], w_gate_up[0], saved_routed[0],
     )
-    routed = routed.transpose(1, 0, 2).reshape(tok, HR)
-    shared = shared.transpose(1, 0, 2).reshape(tok, HR)
-    return (routed + shared).astype(bf), gates[:, :TOP]
+    return grad_in, gates.T
 
 
 def solution(mesh):

time: 73.2 us -> 64.3 us (0.88)
  local copies, waits for them, and re-layouts: 9.38 us -> 2.72 us
  other arithmetic: 2 us -> 0 us
    reshape x5 -> x0, local copies, waits for them, and re-layouts: 4.36 us -> none  [the longest x2 1.8 us: per_device(): pieces = grad_out.reshape(tok, E, DS).transpose(1, 0, 2)]
    convert_element_type x2 -> x0, other arithmetic: 1.33 us -> none  [the longest x1 0.69 us: per_device(): expert_ids.astype(jnp.float32)]
    unnamed x3 -> x2, local copies, waits for them, and re-layouts: 3.88 us -> 2.72 us
    transpose x1 -> x0, local copies, waits for them, and re-layouts: 0.98 us -> none  [per_device(): shared = shared.transpose(1, 0, 2).reshape(tok, HR)]
where the time goes in v2:
time: 64.3 us; the launch traced here: 64.1 us
  Pallas kernels  60.7 us (94%)
  local copies, waits for them, and re-layouts  2.72 us (4%)
    pallas_call x1, Pallas kernels, per_device(): pl.pallas_call(functools.partial(kernel, E, T, F, NC, TOP), out_shape=(ja...  60.7 us
    unnamed x2, local copies, waits for them, and re-layouts  2.72 us

profile of v2, /device:TPU:0, one launch (start us, length us, event | category | flops | bytes accessed | tf_op | source)
XLA Modules:
  0.0 64.1 jit_solution(10476375494548545266)
XLA Ops:
  0.6 60.7 %shard_map.104 = (bf16[16,1792]{1,0:T(8,128)(2,1)}, f32[8,16]{1,0:T(8,128)}) custom-call(bf16[16,3584]{1,0:T(8,128)(2,1)} %g_ref.1, s32[8,16]{1,0:T(8,128)} %bitcast.11, f32[8,16]{1,0:T(8,128)} %bitcast.12, bf16[2,16,512]{2,1,0:T(8,128)(2,1)} %sv_ref.1, bf16[2,224,512]{2,1,0:T(8,128)(2,1)} %sgu_ref.1, bf16[224,512]{1,0:T(8,128)(2,1)} %bitcast.10, ...), custom_call_target="tpu_custom_call" | custom-call | tf_op jit(solution)/shard_map/pallas_call | solution.py:454
  61.4 1.4 %copy.13 = bf16[16,1792]{1,0:T(8,128)(2,1)} copy(bf16[16,1792]{1,0:T(8,128)(2,1)} %get-tuple-element.8) | data formatting | bytes 114688
  62.8 1.3 %copy.14 = f32[16,8]{0,1:T(8,128)} copy(f32[16,8]{0,1:T(8,128)} %bitcast.13) | data formatting | bytes 1024

commit v3 on v2

v3 whole, which is shorter than its diff:
```python
import functools

import jax
import jax.numpy as jnp
from jax import lax
from jax.experimental import pallas as pl
from jax.experimental.pallas import tpu as pltpu
from jax.sharding import PartitionSpec as P

MESH = pl.DeviceIdType.MESH
LANES = 128


def dot_nt(left, right):
    return lax.dot_general(
        left, right, (((1,), (1,)), ((), ())), preferred_element_type=jnp.float32
    )


def loop(count, body):
    def step(i, carry):
        body(i)
        return carry

    lax.fori_loop(0, count, step, 0)


def flat(value):
    return value.reshape(-1, value.shape[-1])


def kernel(
    E, T, F, NC, TOP,
    g_ref, id_ref, gv_ref, sv_ref, sd_hbm, sr_hbm, wd_hbm, sgu_hbm, wgu_hbm,
    out_r, out_g,
    x_ref, square, spread, gbuf, xbuf, sd, sr, wd, sgu, wgu,
    ps, q3buf, q2buf, qzbuf, s3buf, st, s4buf, s4pair,
    pairsend, pairbuf, part, r3buf, r2buf, rzbuf,
    wsem, g_recv, g_sz, g_s2, g_s3, g_ps, g_pr,
    s3_recv, s3_sz, s3_s2, s3_s3,
    x_s, x_r, s4_s, s4_r, s4p_s, s4p_r, pair_s, pair_r,
    r3_s, r3_r, r2_s, r2_r, rz_s, rz_r,
    q3_s, q3_r, q2_s, q2_r, qz_s, qz_r,
):
    me = lax.axis_index("expert")
    j = lax.axis_index("tensor")
    A = E // 4
    a = me // 4
    r = me % 4
    rc = r + 1 - 2 * (r % 2)
    rb = r + 2 - 4 * (r // 2)
    odd = j % 2
    r2 = rc * (1 - odd) + rb * odd
    r3 = rb * (1 - odd) + rc * odd
    r23 = 3 - r
    p2 = a * 4 + r2
    p3 = a * 4 + r3
    fj = j if F > 1 else 0
    tok = x_ref.shape[1]
    DS = x_ref.shape[2]
    FFl = wd.shape[0]
    H = gbuf.shape[3] - LANES
    own_g = gbuf.at[fj, me]
    HC = part.shape[3] - LANES
    HR = HC * NC
    tokens = E * tok

    def rc_(src, dst, ssem, rsem, chip, core):
        return pltpu.make_async_remote_copy(
            src_ref=src, dst_ref=dst, send_sem=ssem, recv_sem=rsem,
            device_id=(chip, core), device_id_type=MESH,
        )

    wcopies = [
        pltpu.make_async_copy(sd_hbm, sd, wsem.at[0]),
        pltpu.make_async_copy(sr_hbm, sr, wsem.at[1]),
        pltpu.make_async_copy(wd_hbm, wd, wsem.at[2]),
        pltpu.make_async_copy(sgu_hbm, sgu, wsem.at[3]),
        pltpu.make_async_copy(wgu_hbm, wgu, wsem.at[4]),
    ]
    for copy in wcopies:
        copy.start()

    barrier = pltpu.get_barrier_semaphore()

    def greet(i):
        pl.semaphore_signal(barrier, inc=1, device_id=((me + i + 1) % E, j), device_id_type=MESH)

    loop(E - 1, greet)
    for d in range(1, T):
        pl.semaphore_signal(barrier, inc=1, device_id=(me, (j + d) % T), device_id_type=MESH)

    for o in range(E):
        x_ref[o] = g_ref[:, o * DS:(o + 1) * DS]
    square[...] = jnp.zeros_like(square)
    square[0:TOP, 0:tok] = id_ref[...].astype(jnp.float32)
    high = gv_ref[...].astype(jnp.bfloat16).astype(jnp.float32)
    square[TOP:2 * TOP, 0:tok] = high
    square[2 * TOP:3 * TOP, 0:tok] = gv_ref[...] - high
    own_meta = square[...].T[0:tok]
    gbuf[fj, me, :, 0:LANES] = own_meta.astype(jnp.bfloat16)
    if F > 1:
        gbuf[fj, me, :, LANES:] = g_ref[:, pl.ds(pl.multiple_of(fj * H, LANES), H)]
    else:
        gbuf[fj, me, :, LANES:] = g_ref[...]

    pl.semaphore_wait(barrier, E - 1 + T - 1)

    def a2a_send(src_of, dst, ssem, rsem):
        def body(i):
            o = (me + i + 1) % E
            rc_(src_of(o), dst.at[me], ssem.at[o], rsem.at[me], o, j).start()

        loop(E - 1, body)

    def a2a_wait(dst, rsem):
        def body(i):
            o = (me + i + 1) % E
            rc_(dst.at[o], dst.at[o], rsem.at[o], rsem.at[o], o, j).wait_recv()

        loop(E - 1, body)

    def a2a_drain(src_of, ssem):
        def body(i):
            o = (me + i + 1) % E
            rc_(src_of(o), src_of(o), ssem.at[o], ssem.at[o], o, j).wait_send()

        loop(E - 1, body)

    class Tree:
        def __init__(self, buf, own, recv, sz, s2, s3, hook):
            self.buf, self.own, self.recv = buf, own, recv
            self.sz, self.s2, self.s3, self.hook = sz, s2, s3, hook

        def send(self, blk, ssem, chip, src=None):
            src = self.buf.at[blk] if src is None else src
            rc_(src, self.buf.at[blk], ssem, self.recv.at[blk], chip, j).start()

        def wait(self, blk):
            rc_(self.buf.at[blk], self.buf.at[blk], self.recv.at[blk], self.recv.at[blk], p2, j).wait_recv()

        def start(self):
            self.send(me, self.s3.at[0], p3, self.own)
            self.send(me, self.s2.at[0], p2, self.own)

            def body(i):
                self.send(me, self.sz.at[i], ((a + i + 1) % A) * 4 + r, self.own)

            loop(A - 1, body)
            self.hook(me, self.own)

        def stage_z(self):
            def body(i):
                blk = ((a + i + 1) % A) * 4 + r
                self.wait(blk)
                self.send(blk, self.s3.at[i + 1], p3)
                self.send(blk, self.s2.at[i + 1], p2)
                self.hook(blk, self.buf.at[blk])

            loop(A - 1, body)

        def stage_2(self):
            def body(i):
                blk = ((a + i) % A) * 4 + r2
                self.wait(blk)
                self.send(blk, self.s3.at[A + i], p3)
                self.hook(blk, self.buf.at[blk])

            loop(A, body)

        def stage_3(self):
            for rr in (r3, r23):
                def body(i):
                    blk = ((a + i) % A) * 4 + rr
                    self.wait(blk)
                    self.hook(blk, self.buf.at[blk])

                loop(A, body)

        def drain(self):
            def one(sem):
                rc_(self.own, self.own, sem, sem, p2, j).wait_send()

            loop(A - 1, lambda i: one(self.sz.at[i]))
            loop(A, lambda i: one(self.s2.at[i]))
            loop(2 * A, lambda i: one(self.s3.at[i]))

    class Reduce:
        def __init__(self, part, b3, b2, bz, s3, v3, s2, v2, sz, vz):
            self.part, self.b3, self.b2, self.bz = part, b3, b2, bz
            self.s3, self.v3, self.s2, self.v2, self.sz, self.vz = s3, v3, s2, v2, sz, vz

        def copy3(self, i):
            first = 1 - i // A
            blk = (i % A) * 4 + r23 * first + r3 * (1 - first)
            return rc_(self.part.at[blk], self.b3.at[i], self.s3.at[i], self.v3.at[i], p3, j)

        def copy2(self, i):
            return rc_(self.part.at[i * 4 + r2], self.b2.at[i], self.s2.at[i], self.v2.at[i], p2, j)

        def copyz(self, o):
            return rc_(
                self.part.at[o * 4 + r], self.bz.at[a], self.sz.at[o], self.vz.at[a], o * 4 + r, j
            )

        def start(self):
            loop(2 * A, lambda i: self.copy3(i).start())

        def stage_2(self):
            def body(i):
                self.copy3(i).wait_recv()
                blk = i * 4 + r2
                self.part[blk] = (
                    self.part[blk].astype(jnp.float32) + self.b3[i].astype(jnp.float32)
                ).astype(jnp.bfloat16)
                self.copy2(i).start()

            loop(A, body)

        def stage_z(self):
            def total(o):
                self.copy3(A + o).wait_recv()
                self.copy2(o).wait_recv()
                return (
                    self.part[o * 4 + r].astype(jnp.float32)
                    + self.b3[A + o].astype(jnp.float32)
                    + self.b2[o].astype(jnp.float32)
                ).astype(jnp.bfloat16)

            def body(i):
                o = (a + i + 1) % A
                self.part[o * 4 + r] = total(o)
                self.copyz(o).start()

            loop(A - 1, body)
            self.bz[a] = total(a)

        def finish(self):
            def body(i):
                o = (a + i + 1) % A
                rc_(self.bz.at[o], self.bz.at[o], self.sz.at[o], self.vz.at[o], p2, j).wait_recv()

            loop(A - 1, body)
            out = self.bz[0].astype(jnp.float32)
            for i in range(1, A):
                out = out + self.bz[i].astype(jnp.float32)
            return out

        def drain(self):
            loop(2 * A, lambda i: self.copy3(i).wait_send())
            loop(A, lambda i: self.copy2(i).wait_send())
            loop(A - 1, lambda i: self.copyz((a + i + 1) % A).wait_send())

    def pair_hook(blk, src):
        if F > 1:
            for d in range(1, T):
                rc_(
                    src, gbuf.at[j, blk], g_ps.at[d, blk], g_pr.at[j, blk], me, (j + d) % T
                ).start()

    tree_g = Tree(gbuf.at[fj], own_g, g_recv, g_sz, g_s2, g_s3, pair_hook)
    tree_s = Tree(s3buf, s3buf.at[me], s3_recv, s3_sz, s3_s2, s3_s3, lambda blk, src: None)

    red_q = Reduce(ps, q3buf, q2buf, qzbuf, q3_s, q3_r, q2_s, q2_r, qz_s, qz_r)
    red_r = []
    for c in range(NC):
        cols = pl.ds(0, LANES + HC) if c == 0 else pl.ds(LANES, HC)
        red_r.append(
            Reduce(
                part.at[c, :, :, cols], r3buf.at[c, :, :, cols], r2buf.at[c, :, :, cols],
                rzbuf.at[c, :, :, cols], r3_s.at[c], r3_r.at[c], r2_s.at[c], r2_r.at[c],
                rz_s.at[c], rz_r.at[c],
            )
        )

    a2a_send(lambda o: x_ref.at[o], xbuf, x_s, x_r)
    tree_g.start()
    xbuf[me] = x_ref[me]

    wcopies[0].wait()
    a2a_wait(xbuf, x_r)
    partial = jnp.dot(flat(xbuf[...]), sd[...], preferred_element_type=jnp.float32)
    ps[...] = partial.astype(jnp.bfloat16).reshape(E, tok, FFl)
    red_q.start()

    tree_g.stage_z()
    red_q.stage_2()
    tree_g.stage_2()
    red_q.stage_z()
    tree_g.stage_3()

    shared_back = red_q.finish()
    sh = sv_ref[0].astype(jnp.float32)
    su = sv_ref[1].astype(jnp.float32)
    ssig = jax.nn.sigmoid(sh)
    s3buf[me, 0] = (shared_back * su * ssig * (1.0 + sh * (1.0 - ssig))).astype(jnp.bfloat16)
    s3buf[me, 1] = (shared_back * sh * ssig).astype(jnp.bfloat16)
    tree_s.start()

    meta = flat(gbuf[fj, :, :, 0:LANES]).astype(jnp.float32)
    lane = lax.broadcasted_iota(jnp.int32, (tokens, LANES), 1)
    hit = jnp.where((meta == me.astype(jnp.float32)) & (lane < TOP), 1.0, 0.0)
    gates = pltpu.roll(meta, LANES - TOP, 1) + pltpu.roll(meta, LANES - 2 * TOP, 1)
    chosen = jnp.sum(hit, axis=1, keepdims=True)
    gate = jnp.sum(hit * gates, axis=1, keepdims=True)
    wide = jnp.broadcast_to(chosen, (tokens, LANES))
    row = lax.broadcasted_iota(jnp.int32, (tokens, LANES), 0) % tok
    total = wide
    shift = 1
    while shift < tok:
        total = total + jnp.where(row >= shift, pltpu.roll(total, shift, 0), 0.0)
        shift *= 2
    position = (total - wide)[:, :1]
    slots = sr.shape[1]
    cap = slots // E
    base = (lax.broadcasted_iota(jnp.int32, (tokens, 1), 0) // tok) * cap
    target = position + base.astype(jnp.float32)
    slot = lax.broadcasted_iota(jnp.int32, (tokens, slots), 1).astype(jnp.float32)
    permute = jnp.where((slot == target) & (chosen > 0.5), 1.0, 0.0).astype(jnp.bfloat16)
    wcopies[1].wait()
    pre_gate = jnp.dot(permute, sr[0], preferred_element_type=jnp.float32)
    pre_up = jnp.dot(permute, sr[1], preferred_element_type=jnp.float32)
    sig = jax.nn.sigmoid(pre_gate)
    d_up = pre_gate * sig
    d_gate = pre_up * sig * (1.0 + pre_gate * (1.0 - sig))

    wcopies[2].wait()

    def back_of(t):
        return dot_nt(flat(gbuf[t, :, :, LANES:]), wd[:, pl.ds(pl.multiple_of(t * H, LANES), H)])

    if F > 1:
        back = back_of(j)
        for d in range(1, T):
            other = (j + d) % T

            def body(i):
                ref = gbuf.at[other, i]
                rc_(ref, ref, g_pr.at[other, i], g_pr.at[other, i], me, other).wait_recv()

            loop(E, body)
            back = back + back_of(other)
    else:
        back = dot_nt(flat(gbuf[0, :, :, LANES:]), wd[...])
    tree_s.stage_z()
    grad_up = back * d_up
    gate_sum = jnp.sum(grad_up * pre_up, axis=1, keepdims=True)
    grad_gate = (back * d_gate * gate).astype(jnp.bfloat16)
    grad_up = (grad_up * gate).astype(jnp.bfloat16)
    place = j * E + me if T * E <= LANES else me
    gate_row = jnp.where(lane == place, gate_sum, 0.0).astype(jnp.bfloat16)

    wcopies[4].wait()

    def rows_of(t, c):
        span = pl.ds(pl.multiple_of(t * HR + c * HC, 16), HC)
        return dot_nt(grad_gate, wgu[0, span, :]) + dot_nt(grad_up, wgu[1, span, :])

    for c in range(NC):
        for d in range(1, T):
            t = (j + d) % T
            pairsend[d - 1, c, :, LANES:] = rows_of(t, c).astype(jnp.bfloat16)
            if c == 0:
                pairsend[d - 1, c, :, 0:LANES] = gate_row
            rc_(
                pairsend.at[d - 1, c], pairbuf.at[T - 1 - d, c],
                pair_s.at[d - 1, c], pair_r.at[T - 1 - d, c], me, t,
            ).start()

    tree_s.stage_2()

    for c in range(NC):
        mine = rows_of(j, c)
        for d in range(1, T):
            rc_(
                pairsend.at[d - 1, c], pairbuf.at[d - 1, c],
                pair_s.at[d - 1, c], pair_r.at[d - 1, c], me, (j + d) % T,
            ).wait_recv()
            mine = mine + pairbuf[d - 1, c, :, LANES:].astype(jnp.float32)
        part[c, :, :, LANES:] = mine.astype(jnp.bfloat16).reshape(E, tok, HC)
        if c == 0:
            sums = gate_row.astype(jnp.float32)
            for d in range(1, T):
                sums = sums + pairbuf[d - 1, c, :, 0:LANES].astype(jnp.float32)
            part[c, :, :, 0:LANES] = sums.astype(jnp.bfloat16).reshape(E, tok, LANES)
        red_r[c].start()

    tree_s.stage_3()
    wcopies[3].wait()
    term = dot_nt(flat(s3buf[:, 0]), sgu[0]) + dot_nt(flat(s3buf[:, 1]), sgu[1])
    st[...] = term.astype(jnp.bfloat16).reshape(E, tok, st.shape[2])
    a2a_send(lambda o: st.at[o], s4buf, s4_s, s4_r)
    s4buf[me] = st[me]

    a2a_drain(lambda o: x_ref.at[o], x_s)
    tree_g.drain()
    red_q.drain()
    if F > 1:
        for d in range(1, T):
            loop(
                E,
                lambda i: rc_(
                    gbuf.at[j, i], gbuf.at[j, i], g_ps.at[d, i], g_ps.at[d, i], me, (j + d) % T
                ).wait_send(),
            )

    for c in range(NC):
        red_r[c].stage_2()
        red_r[c].stage_z()
    tree_s.drain()

    a2a_wait(s4buf, s4_r)
    group = E // T
    for d in range(1, T):
        t = (j + d) % T
        rc_(
            s4buf.at[pl.ds(t * group, group)], s4pair.at[T - 1 - d],
            s4p_s.at[d - 1], s4p_r.at[T - 1 - d], me, t,
        ).start()
    shared = s4buf[pl.ds(j * group, group)].astype(jnp.float32)
    for d in range(1, T):
        rc_(
            s4pair.at[d - 1], s4pair.at[d - 1], s4p_s.at[d - 1], s4p_r.at[d - 1], me, (j + d) % T
        ).wait_recv()
        shared = shared + s4pair[d - 1].astype(jnp.float32)
    for o in range(group):
        spread[:, o * DS:(o + 1) * DS] = shared[o]
    a2a_drain(lambda o: st.at[o], s4_s)
    for d in range(1, T):
        rc_(
            s4pair.at[d - 1], s4pair.at[d - 1], s4p_s.at[d - 1], s4p_s.at[d - 1], me, (j + d) % T
        ).wait_send()
        for c in range(NC):
            ref = pairsend.at[d - 1, c]
            rc_(ref, ref, pair_s.at[d - 1, c], pair_s.at[d - 1, c], me, (j + d) % T).wait_send()

    done = [red_r[c].finish() for c in range(NC)]
    for c in range(NC):
        rows = done[c][:, LANES:] if c == 0 else done[c]
        out_r[:, c * HC:(c + 1) * HC] = rows + spread[:, c * HC:(c + 1) * HC]
    sums = done[0][:, 0:LANES]
    lane16 = lax.broadcasted_iota(jnp.int32, (tok, LANES), 1)
    expert_f = (lane16 % E).astype(jnp.float32)
    for parity in range(2):
        some = jnp.where(lane16 % 2 == parity, sums, 0.0)
        result = jnp.zeros((tok, LANES), jnp.float32)
        for k in range(TOP):
            value = jnp.sum(
                jnp.where(expert_f == own_meta[:, k:k + 1], some, 0.0), axis=1, keepdims=True
            )
            result = jnp.where(lane16 == k, value, result)
        square[0:tok] = result
        out_g[parity] = square[...].T[0:TOP, 0:tok]
    for c in range(NC):
        red_r[c].drain()


def per_device(
    E, T,
    grad_out, expert_ids, gate_values, w_gate_up, w_down, saved_routed,
    shared_gate_up, shared_down, saved_shared,
):
    tok, D = grad_out.shape
    TOP = expert_ids.shape[1]
    FFl = w_down.shape[1]
    DS = shared_down.shape[1]
    slots = saved_routed.shape[2]
    F = T if (D // T) % LANES == 0 else 1
    H = D // F
    HR = D // T
    NC = 2 if HR % (2 * LANES) == 0 else 1
    HC = HR // NC
    A = E // 4
    tokens = E * tok
    bf, f32 = jnp.bfloat16, jnp.float32
    V, S = pltpu.VMEM, pltpu.SemaphoreType.DMA
    T1 = max(T - 1, 1)
    W = LANES + HC
    scratch = [
        V((E, tok, DS), bf), V((LANES, LANES), f32), V((tok, HR), f32),
        V((F, E, tok, LANES + H), bf), V((E, tok, DS), bf),
        V((DS, FFl), bf), V((2, slots, FFl), bf), V((FFl, D), bf), V((2, DS, FFl), bf), V((2, D, FFl), bf),
        V((E, tok, FFl), bf), V((2 * A, tok, FFl), bf), V((A, tok, FFl), bf), V((A, tok, FFl), bf),
        V((E, 2, tok, FFl), bf),
        V((E, tok, DS), bf), V((E, tok, DS), bf), V((T1, E // T, tok, DS), bf),
        V((T1, NC, tokens, W), bf), V((T1, NC, tokens, W), bf), V((NC, E, tok, W), bf),
        V((NC, 2 * A, tok, W), bf), V((NC, A, tok, W), bf), V((NC, A, tok, W), bf),
        S((5,)), S((E,)), S((A,)), S((A,)), S((2 * A,)), S((T, E)), S((T, E)),
        S((E,)), S((A,)), S((A,)), S((2 * A,)),
        S((E,)), S((E,)), S((E,)), S((E,)), S((T1,)), S((T1,)), S((T1, NC)), S((T1, NC)),
        S((NC, 2 * A)), S((NC, 2 * A)), S((NC, A)), S((NC, A)), S((NC, A)), S((NC, A)),
        S((2 * A,)), S((2 * A,)), S((A,)), S((A,)), S((A,)), S((A,)),
    ]
    vm = pl.BlockSpec(memory_space=pltpu.VMEM)
    hbm = pl.BlockSpec(memory_space=pltpu.HBM)
    grad_in, gates = pl.pallas_call(
        functools.partial(kernel, E, T, F, NC, TOP),
        out_shape=(
            jax.ShapeDtypeStruct((tok, HR), f32),
            jax.ShapeDtypeStruct((2, TOP, tok), f32),
        ),
        in_specs=[vm] * 4 + [hbm] * 5,
        out_specs=(vm, vm),
        scratch_shapes=scratch,
        compiler_params=pltpu.CompilerParams(
            collective_id=0, has_side_effects=True, vmem_limit_bytes=60 * 1024 * 1024
        ),
    )(
        grad_out, expert_ids.T, gate_values.T, saved_shared, shared_down.T, saved_routed[0],
        w_down[0], shared_gate_up, w_gate_up[0],
    )
    return grad_in.astype(bf), (gates[0] + gates[1]).T


def solution(mesh):
    return jax.shard_map(
        functools.partial(per_device, mesh.shape["expert"], mesh.shape["tensor"]),
        mesh=mesh,
        in_specs=(
            P("expert", None),
            P("expert", None),
            P("expert", None),
            P("expert", None, None, "tensor"),
            P("expert", "tensor", None),
            P("expert", None, None, "tensor"),
            P(None, "expert", "tensor"),
            P("tensor", "expert"),
            P(None, "expert", "tensor"),
        ),
        out_specs=(P("expert", "tensor"), P("expert", None)),
        check_vma=False,
    )
```

time: 64.3 us -> 59.2 us (0.921)
  Pallas kernels: 60.7 us -> 55.5 us
  other arithmetic: 0 us -> 2.81 us
  local copies, waits for them, and re-layouts: 2.72 us -> 0 us
    pallas_call x1, Pallas kernels: 60.7 us -> 55.5 us  [per_device(): pl.pallas_call(functools.partial(kernel, E, T, F, NC, TOP), out_shape=(ja...]
    unnamed x2 -> x0, local copies, waits for them, and re-layouts: 2.72 us -> none
    convert_element_type x0 -> x1, other arithmetic: none -> 1.53 us  [per_device(): return (grad_in.astype(bf), (gates[0] + gates[1]).T)]
    transpose x0 -> x1, other arithmetic: none -> 1.28 us  [per_device(): return (grad_in.astype(bf), (gates[0] + gates[1]).T)]
where the time goes in v3:
time: 59.2 us; the launch traced here: 59 us
  Pallas kernels  55.5 us (94%)
  other arithmetic  2.81 us (5%)
  between operations  0.64 us (1%)
    pallas_call x1, Pallas kernels, per_device(): pl.pallas_call(functools.partial(kernel, E, T, F, NC, TOP), out_shape=(ja...  55.5 us
    convert_element_type x1, other arithmetic, per_device(): return (grad_in.astype(bf), (gates[0] + gates[1]).T)  1.53 us
    transpose x1, other arithmetic, per_device(): return (grad_in.astype(bf), (gates[0] + gates[1]).T)  1.28 us

profile of v3, /device:TPU:0, one launch (start us, length us, event | category | flops | bytes accessed | tf_op | source)
XLA Modules:
  0.0 59.0 jit_solution(1434940059331826711)
XLA Ops:
  0.6 55.5 %shard_map.104 = (f32[16,1792]{1,0:T(8,128)}, f32[2,8,16]{2,1,0:T(8,128)}) custom-call(bf16[16,3584]{1,0:T(8,128)(2,1)} %g_ref.1, s32[8,16]{1,0:T(8,128)} %bitcast.14, f32[8,16]{1,0:T(8,128)} %bitcast.15, bf16[2,16,512]{2,1,0:T(8,128)(2,1)} %sv_ref.1, bf16[224,512]{1,0:T(8,128)(2,1)} %bitcast.13, bf16[2,256,512]{2,1,0:T(8,128)(2,1)} %bitcast.12, ...), custom_call_target="tpu_custom_call" | custom-call | tf_op jit(solution)/shard_map/pallas_call | solution.py:496
  56.2 1.5 %convert_element_type.3 = bf16[16,1792]{1,0:T(8,128)(2,1)} convert(f32[16,1792]{1,0:T(8,128)} %get-tuple-element.4) | non-fusion elementwise | flops 28672 | bytes 172032 | tf_op jit(solution)/shard_map/convert_element_type | solution.py:512
  57.7 1.3 %add_bitcast_fusion = f32[16,8]{0,1:T(8,128)} fusion(f32[2,8,16]{2,1,0:T(8,128)} %get-tuple-element.5), kind=kLoop, calls=%fused_computation | loop fusion | flops 128 | bytes 1536 | tf_op jit(solution)/shard_map/transpose | solution.py:512

commit v4 on v3

--- a/solution.py
+++ b/solution.py
@@ -33,12 +33,12 @@
     E, T, F, NC, TOP,
     g_ref, id_ref, gv_ref, sv_ref, sd_hbm, sr_hbm, wd_hbm, sgu_hbm, wgu_hbm,
     out_r, out_g,
-    x_ref, square, spread, gbuf, xbuf, sd, sr, wd, sgu, wgu,
+    square, spread, gbuf, sd, sdpad, sr, wd, sgu, wgu,
     ps, q3buf, q2buf, qzbuf, s3buf, st, s4buf, s4pair,
     pairsend, pairbuf, part, r3buf, r2buf, rzbuf,
     wsem, g_recv, g_sz, g_s2, g_s3, g_ps, g_pr,
     s3_recv, s3_sz, s3_s2, s3_s3,
-    x_s, x_r, s4_s, s4_r, s4p_s, s4p_r, pair_s, pair_r,
+    s4_s, s4_r, s4p_s, s4p_r, pair_s, pair_r,
     r3_s, r3_r, r2_s, r2_r, rz_s, rz_r,
     q3_s, q3_r, q2_s, q2_r, qz_s, qz_r,
 ):
@@ -56,8 +56,8 @@
     p2 = a * 4 + r2
     p3 = a * 4 + r3
     fj = j if F > 1 else 0
-    tok = x_ref.shape[1]
-    DS = x_ref.shape[2]
+    tok = g_ref.shape[0]
+    DS = sd.shape[0]
     FFl = wd.shape[0]
     H = gbuf.shape[3] - LANES
     own_g = gbuf.at[fj, me]
@@ -90,8 +90,7 @@
     for d in range(1, T):
         pl.semaphore_signal(barrier, inc=1, device_id=(me, (j + d) % T), device_id_type=MESH)
 
-    for o in range(E):
-        x_ref[o] = g_ref[:, o * DS:(o + 1) * DS]
+    sdpad[...] = jnp.zeros_like(sdpad)
     square[...] = jnp.zeros_like(square)
     square[0:TOP, 0:tok] = id_ref[...].astype(jnp.float32)
     high = gv_ref[...].astype(jnp.bfloat16).astype(jnp.float32)
@@ -273,29 +272,33 @@
             )
         )
 
-    a2a_send(lambda o: x_ref.at[o], xbuf, x_s, x_r)
     tree_g.start()
-    xbuf[me] = x_ref[me]
-
+
+    fgroup = E // F
+    offset = LANES + (me % fgroup) * DS
+    WIN = sdpad.shape[0]
+    low = jnp.minimum(offset // LANES, (LANES + H - WIN) // LANES) * LANES
     wcopies[0].wait()
-    a2a_wait(xbuf, x_r)
-    partial = jnp.dot(flat(xbuf[...]), sd[...], preferred_element_type=jnp.float32)
+    sdpad[pl.ds(pl.multiple_of(offset - low, 8), DS), :] = sd[...].astype(jnp.float32)
+
+    tree_g.stage_z()
+    tree_g.stage_2()
+    tree_g.stage_3()
+    for d in range(1, F):
+        other = (j + d) % T
+
+        def arrived(i):
+            ref = gbuf.at[other, i]
+            rc_(ref, ref, g_pr.at[other, i], g_pr.at[other, i], me, other).wait_recv()
+
+        loop(E, arrived)
+
+    window = flat(gbuf[me // fgroup, :, :, pl.ds(pl.multiple_of(low, LANES), WIN)])
+    partial = jnp.dot(
+        window, sdpad[...].astype(jnp.bfloat16), preferred_element_type=jnp.float32
+    )
     ps[...] = partial.astype(jnp.bfloat16).reshape(E, tok, FFl)
     red_q.start()
-
-    tree_g.stage_z()
-    red_q.stage_2()
-    tree_g.stage_2()
-    red_q.stage_z()
-    tree_g.stage_3()
-
-    shared_back = red_q.finish()
-    sh = sv_ref[0].astype(jnp.float32)
-    su = sv_ref[1].astype(jnp.float32)
-    ssig = jax.nn.sigmoid(sh)
-    s3buf[me, 0] = (shared_back * su * ssig * (1.0 + sh * (1.0 - ssig))).astype(jnp.bfloat16)
-    s3buf[me, 1] = (shared_back * sh * ssig).astype(jnp.bfloat16)
-    tree_s.start()
 
     meta = flat(gbuf[fj, :, :, 0:LANES]).astype(jnp.float32)
     lane = lax.broadcasted_iota(jnp.int32, (tokens, LANES), 1)
@@ -334,15 +337,10 @@
         for d in range(1, T):
             other = (j + d) % T
 
-            def body(i):
-                ref = gbuf.at[other, i]
-                rc_(ref, ref, g_pr.at[other, i], g_pr.at[other, i], me, other).wait_recv()
-
-            loop(E, body)
             back = back + back_of(other)
     else:
         back = dot_nt(flat(gbuf[0, :, :, LANES:]), wd[...])
-    tree_s.stage_z()
+    red_q.stage_2()
     grad_up = back * d_up
     gate_sum = jnp.sum(grad_up * pre_up, axis=1, keepdims=True)
     grad_gate = (back * d_gate * gate).astype(jnp.bfloat16)
@@ -367,7 +365,16 @@
                 pair_s.at[d - 1, c], pair_r.at[T - 1 - d, c], me, t,
             ).start()
 
-    tree_s.stage_2()
+    red_q.stage_z()
+
+    def hidden_of_shared():
+        shared_back = red_q.finish()
+        sh = sv_ref[0].astype(jnp.float32)
+        su = sv_ref[1].astype(jnp.float32)
+        ssig = jax.nn.sigmoid(sh)
+        s3buf[me, 0] = (shared_back * su * ssig * (1.0 + sh * (1.0 - ssig))).astype(jnp.bfloat16)
+        s3buf[me, 1] = (shared_back * sh * ssig).astype(jnp.bfloat16)
+        tree_s.start()
 
     for c in range(NC):
         mine = rows_of(j, c)
@@ -384,6 +391,15 @@
                 sums = sums + pairbuf[d - 1, c, :, 0:LANES].astype(jnp.float32)
             part[c, :, :, 0:LANES] = sums.astype(jnp.bfloat16).reshape(E, tok, LANES)
         red_r[c].start()
+        if c == 0:
+            hidden_of_shared()
+
+    red_r[0].stage_2()
+    tree_s.stage_z()
+    red_r[0].stage_z()
+    tree_s.stage_2()
+    if NC > 1:
+        red_r[1].stage_2()
 
     tree_s.stage_3()
     wcopies[3].wait()
@@ -392,7 +408,6 @@
     a2a_send(lambda o: st.at[o], s4buf, s4_s, s4_r)
     s4buf[me] = st[me]
 
-    a2a_drain(lambda o: x_ref.at[o], x_s)
     tree_g.drain()
     red_q.drain()
     if F > 1:
@@ -404,9 +419,8 @@
                 ).wait_send(),
             )
 
-    for c in range(NC):
-        red_r[c].stage_2()
-        red_r[c].stage_z()
+    if NC > 1:
+        red_r[1].stage_z()
     tree_s.drain()
 
     a2a_wait(s4buf, s4_r)
@@ -476,10 +490,11 @@
     V, S = pltpu.VMEM, pltpu.SemaphoreType.DMA
     T1 = max(T - 1, 1)
     W = LANES + HC
+    WIN = (DS + LANES + LANES - 1) // LANES * LANES
     scratch = [
-        V((E, tok, DS), bf), V((LANES, LANES), f32), V((tok, HR), f32),
-        V((F, E, tok, LANES + H), bf), V((E, tok, DS), bf),
-        V((DS, FFl), bf), V((2, slots, FFl), bf), V((FFl, D), bf), V((2, DS, FFl), bf), V((2, D, FFl), bf),
+        V((LANES, LANES), f32), V((tok, HR), f32),
+        V((F, E, tok, LANES + H), bf), V((DS, FFl), bf), V((WIN, FFl), f32),
+        V((2, slots, FFl), bf), V((FFl, D), bf), V((2, DS, FFl), bf), V((2, D, FFl), bf),
         V((E, tok, FFl), bf), V((2 * A, tok, FFl), bf), V((A, tok, FFl), bf), V((A, tok, FFl), bf),
         V((E, 2, tok, FFl), bf),
         V((E, tok, DS), bf), V((E, tok, DS), bf), V((T1, E // T, tok, DS), bf),
@@ -487,7 +502,7 @@
         V((NC, 2 * A, tok, W), bf), V((NC, A, tok, W), bf), V((NC, A, tok, W), bf),
         S((5,)), S((E,)), S((A,)), S((A,)), S((2 * A,)), S((T, E)), S((T, E)),
         S((E,)), S((A,)), S((A,)), S((2 * A,)),
-        S((E,)), S((E,)), S((E,)), S((E,)), S((T1,)), S((T1,)), S((T1, NC)), S((T1, NC)),
+        S((E,)), S((E,)), S((T1,)), S((T1,)), S((T1, NC)), S((T1, NC)),
         S((NC, 2 * A)), S((NC, 2 * A)), S((NC, A)), S((NC, A)), S((NC, A)), S((NC, A)),
         S((2 * A,)), S((2 * A,)), S((A,)), S((A,)), S((A,)), S((A,)),
     ]

time: 59.2 us -> 58.9 us (level)
  no operation moved by 1% of the time
where the time goes in v4:
time: 58.9 us; the launch traced here: 58.5 us
  Pallas kernels  55.1 us (94%)
  other arithmetic  2.81 us (5%)
  between operations  0.64 us (1%)
    pallas_call x1, Pallas kernels, per_device(): pl.pallas_call(functools.partial(kernel, E, T, F, NC, TOP), out_shape=(ja...  55.1 us
    convert_element_type x1, other arithmetic, per_device(): return (grad_in.astype(bf), (gates[0] + gates[1]).T)  1.53 us
    transpose x1, other arithmetic, per_device(): return (grad_in.astype(bf), (gates[0] + gates[1]).T)  1.28 us

profile of v4, /device:TPU:0, one launch (start us, length us, event | category | flops | bytes accessed | tf_op | source)
XLA Modules:
  0.0 58.5 jit_solution(11904134625112538848)
XLA Ops:
  0.6 55.1 %shard_map.104 = (f32[16,1792]{1,0:T(8,128)}, f32[2,8,16]{2,1,0:T(8,128)}) custom-call(bf16[16,3584]{1,0:T(8,128)(2,1)} %g_ref.1, s32[8,16]{1,0:T(8,128)} %bitcast.14, f32[8,16]{1,0:T(8,128)} %bitcast.15, bf16[2,16,512]{2,1,0:T(8,128)(2,1)} %sv_ref.1, bf16[224,512]{1,0:T(8,128)(2,1)} %bitcast.13, bf16[2,256,512]{2,1,0:T(8,128)(2,1)} %bitcast.12, ...), custom_call_target="tpu_custom_call" | custom-call | tf_op jit(solution)/shard_map/pallas_call | solution.py:511
  55.7 1.5 %convert_element_type.3 = bf16[16,1792]{1,0:T(8,128)(2,1)} convert(f32[16,1792]{1,0:T(8,128)} %get-tuple-element.4) | non-fusion elementwise | flops 28672 | bytes 172032 | tf_op jit(solution)/shard_map/convert_element_type | solution.py:527
  57.3 1.3 %add_bitcast_fusion = f32[16,8]{0,1:T(8,128)} fusion(f32[2,8,16]{2,1,0:T(8,128)} %get-tuple-element.5), kind=kLoop, calls=%fused_computation | loop fusion | flops 128 | bytes 1536 | tf_op jit(solution)/shard_map/transpose | solution.py:527

commit v5 on v4

--- a/solution.py
+++ b/solution.py
@@ -376,6 +376,7 @@
         s3buf[me, 1] = (shared_back * sh * ssig).astype(jnp.bfloat16)
         tree_s.start()
 
+    hidden_of_shared()
     for c in range(NC):
         mine = rows_of(j, c)
         for d in range(1, T):
@@ -392,14 +393,10 @@
             part[c, :, :, 0:LANES] = sums.astype(jnp.bfloat16).reshape(E, tok, LANES)
         red_r[c].start()
         if c == 0:
-            hidden_of_shared()
-
+            tree_s.stage_z()
+
+    tree_s.stage_2()
     red_r[0].stage_2()
-    tree_s.stage_z()
-    red_r[0].stage_z()
-    tree_s.stage_2()
-    if NC > 1:
-        red_r[1].stage_2()
 
     tree_s.stage_3()
     wcopies[3].wait()
@@ -408,6 +405,9 @@
     a2a_send(lambda o: st.at[o], s4buf, s4_s, s4_r)
     s4buf[me] = st[me]
 
+    red_r[0].stage_z()
+    if NC > 1:
+        red_r[1].stage_2()
     tree_g.drain()
     red_q.drain()
     if F > 1:

time: 58.9 us -> 62.1 us (1.054)
  Pallas kernels: 55.1 us -> 58.5 us
    pallas_call x1, Pallas kernels: 55.1 us -> 58.5 us  [per_device(): pl.pallas_call(functools.partial(kernel, E, T, F, NC, TOP), out_shape=(ja...]
where the time goes in v5:
time: 62.1 us; the launch traced here: 61.9 us
  Pallas kernels  58.5 us (94%)
  other arithmetic  2.81 us (5%)
  between operations  0.64 us (1%)
    pallas_call x1, Pallas kernels, per_device(): pl.pallas_call(functools.partial(kernel, E, T, F, NC, TOP), out_shape=(ja...  58.5 us
    convert_element_type x1, other arithmetic, per_device(): return (grad_in.astype(bf), (gates[0] + gates[1]).T)  1.53 us
    transpose x1, other arithmetic, per_device(): return (grad_in.astype(bf), (gates[0] + gates[1]).T)  1.28 us

profile of v5, /device:TPU:0, one launch (start us, length us, event | category | flops | bytes accessed | tf_op | source)
XLA Modules:
  0.0 61.9 jit_solution(10502405128762542372)
XLA Ops:
  0.6 58.5 %shard_map.104 = (f32[16,1792]{1,0:T(8,128)}, f32[2,8,16]{2,1,0:T(8,128)}) custom-call(bf16[16,3584]{1,0:T(8,128)(2,1)} %g_ref.1, s32[8,16]{1,0:T(8,128)} %bitcast.14, f32[8,16]{1,0:T(8,128)} %bitcast.15, bf16[2,16,512]{2,1,0:T(8,128)(2,1)} %sv_ref.1, bf16[224,512]{1,0:T(8,128)(2,1)} %bitcast.13, bf16[2,256,512]{2,1,0:T(8,128)(2,1)} %bitcast.12, ...), custom_call_target="tpu_custom_call" | custom-call | tf_op jit(solution)/shard_map/pallas_call | solution.py:511
  59.1 1.5 %convert_element_type.3 = bf16[16,1792]{1,0:T(8,128)(2,1)} convert(f32[16,1792]{1,0:T(8,128)} %get-tuple-element.4) | non-fusion elementwise | flops 28672 | bytes 172032 | tf_op jit(solution)/shard_map/convert_element_type | solution.py:527
  60.6 1.3 %add_bitcast_fusion = f32[16,8]{0,1:T(8,128)} fusion(f32[2,8,16]{2,1,0:T(8,128)} %get-tuple-element.5), kind=kLoop, calls=%fused_computation | loop fusion | flops 128 | bytes 1536 | tf_op jit(solution)/shard_map/transpose | solution.py:527
